TPU v7x, 32 devices: a whole 2x2x4 slice. The times are simulated.
32 devices in a mesh: dp: 8 (over z, core), mp: 4 (over y, x).
Axes of the slice: x: 2, y: 2, z: 4, core: 2. Of those that a mesh axis runs over, the one named last changes fastest.
Arguments:
- patches: bfloat16 [256, 256, 1280], P(('dp', 'mp')), may hold values from -6 to 6
- position: bfloat16 [256, 1280], replicated, may hold values from -3 to 3
- keep: int32 [256, 64], P(('dp', 'mp')), may hold values from 0 to 255, as said below
- counts: int32 [256], replicated, may hold values from 1 to 64, as said below
- offsets: int32 [256], replicated, may hold values from 0 to 10239, as said below
- ln_gain: float32 [1, 2, 1280], replicated, may hold values from 0.25 to 1.75
- ln_bias: float32 [1, 2, 1280], replicated, may hold values from -2 to 2
- w_qkv: bfloat16 [1, 3, 1280, 1280], P(None, None, 'dp', 'mp')
- b_qkv: float32 [1, 3, 1280], P(None, None, 'mp'), may hold values from -3 to 3
- w_o: bfloat16 [1, 1280, 1280], P(None, 'mp', 'dp'), may hold values from -0.15625 to 0.15625
- b_o: float32 [1, 1280], replicated, may hold values from -1.5 to 1.5
- w_up: bfloat16 [1, 1280, 5120], P(None, 'dp', 'mp'), may hold values from -0.15625 to 0.15625
- b_up: float32 [1, 5120], P(None, 'mp'), may hold values from -3 to 3
- w_down: bfloat16 [1, 5120, 1280], P(None, 'mp', 'dp'), may hold values from -0.078125 to 0.078125
- b_down: float32 [1, 1280], replicated, may hold values from -1.5 to 1.5
Outputs:
- encoded: bfloat16 [10240, 1280], P(('dp', 'mp'))
Inputs may be any that keep to these rules, and one draw needn't show every extreme that they name: `keep`: the first counts[i] entries of row i are distinct and name image i's visible patches; later entries are unused. `counts`: some image has exactly 64 visible patches. Image i, held by dp index s = i // 32, occupies packed rows offsets[i] to offsets[i] + counts[i] - 1, all inside the aligned block of 160 rows numbered d * 8 + s for some shard d; no two images share a row.
All inputs are finite; a program needn't handle non-finite values.
Results may differ from a plain program's by a relative error of at most 0.015.
Values may be sent and summed in bfloat16 or wider, within the bound.
A program may use at most 64 MiB of HBM per device.

v0:
```python
import math

import jax
import jax.numpy as jnp
from jax import lax
from jax.sharding import PartitionSpec as P

HEAD = 80


def norm_rows(values, gain_row, shift_row):
    row_mean = jnp.mean(values, axis=-1, keepdims=True)
    centred = values - row_mean
    spread = jnp.mean(centred * centred, axis=-1, keepdims=True)
    return (centred * lax.rsqrt(spread + 1e-06) * gain_row + shift_row).astype(jnp.bfloat16)


def gather_rows(normed):
    return lax.all_gather(normed, "mp", axis=0, tiled=True)


def fold_rows(gathered, weight):
    return jnp.einsum(
        "rd,tdc->trc",
        gathered,
        lax.all_gather(weight, "dp", axis=1, tiled=True),
        preferred_element_type=jnp.float32,
    )


def project_sum(left, weight):
    partials = jnp.dot(
        left, lax.all_gather(weight, "dp", axis=1, tiled=True), preferred_element_type=jnp.float32
    )
    return lax.psum_scatter(
        partials.astype(jnp.bfloat16), "mp", scatter_dimension=0, tiled=True
    ).astype(jnp.float32)


def attend(projected, labels, block_rows):
    row_count = projected.shape[1]
    blocks = row_count // block_rows
    head_count = projected.shape[2] // HEAD
    shaped = projected.reshape(3, blocks, block_rows, head_count, HEAD)
    scores = jnp.einsum(
        "bqhe,bkhe->bhqk", shaped[0], shaped[1], preferred_element_type=jnp.float32
    ) * (1.0 / math.sqrt(HEAD))
    labels_block = labels.reshape(blocks, block_rows)
    matches = labels_block[:, None, :, None] == labels_block[:, None, None, :]
    scores = jnp.where(matches, scores, -jnp.inf)
    row_max = jnp.max(scores, axis=-1, keepdims=True)
    weights = jnp.exp(scores - row_max)
    probabilities = (weights / jnp.sum(weights, axis=-1, keepdims=True)).astype(jnp.bfloat16)
    attended = jnp.einsum(
        "bhqk,bkhe->bqhe", probabilities, shaped[2], preferred_element_type=jnp.float32
    )
    return attended.reshape(row_count, head_count * HEAD).astype(jnp.bfloat16)


def group_rows(item_count, unit_rows):
    factor = 1
    while item_count % (factor * 2) == 0 and factor * unit_rows < 512:
        factor = factor * 2
    return factor * unit_rows


def run_layers(
    stream, labels, block_rows, ln_gain, ln_bias, w_qkv, b_qkv, w_o, b_o, w_up, b_up, w_down, b_down
):
    normed = norm_rows(stream.astype(jnp.float32), ln_gain[0, 0], ln_bias[0, 0])
    projected = (fold_rows(gather_rows(normed), w_qkv[0]) + b_qkv[0][:, None, :]).astype(
        jnp.bfloat16
    )
    attended = attend(projected, labels, block_rows)
    residual = stream.astype(jnp.float32) + project_sum(attended, w_o[0]) + b_o[0]
    normed_mlp = norm_rows(residual, ln_gain[0, 1], ln_bias[0, 1])
    up_proj = fold_rows(gather_rows(normed_mlp), w_up[0][None])[0] + b_up[0]
    hidden = jax.nn.gelu(up_proj, approximate=False).astype(jnp.bfloat16)
    stream = (residual + project_sum(hidden, w_down[0]) + b_down[0]).astype(jnp.bfloat16)
    return stream


def per_device(
    patches,
    position,
    keep,
    counts,
    offsets,
    ln_gain,
    ln_bias,
    w_qkv,
    b_qkv,
    w_o,
    b_o,
    w_up,
    b_up,
    w_down,
    b_down,
):
    local_images = patches.shape[0]
    keep_most = keep.shape[1]
    column_count = patches.shape[2]
    shard_count = lax.axis_size("dp")
    group_size = lax.axis_size("mp")
    images_here = local_images * group_size
    per_slot = (images_here + shard_count - 1) // shard_count
    slot_rows = max(keep_most + 16, per_slot * keep_most * 5 // 8)
    pack_rows = slot_rows * shard_count
    local_rows = pack_rows // group_size
    dp_index = lax.axis_index("dp")
    mp_index = lax.axis_index("mp")
    first_image = dp_index * images_here
    group_counts = lax.dynamic_slice_in_dim(counts, first_image, images_here)
    group_offsets = lax.dynamic_slice_in_dim(offsets, first_image, images_here)
    picked = jnp.take_along_axis(patches, keep[:, :, None], axis=1)
    placed = jnp.take(position, keep, axis=0)
    tokens = (picked.astype(jnp.float32) + placed.astype(jnp.float32)).astype(jnp.bfloat16)
    positions_in = jnp.arange(keep_most, dtype=jnp.int32)
    group_live = positions_in[None, :] < group_counts[:, None]
    shard_index = group_offsets // pack_rows
    base_row = (
        shard_index * slot_rows + group_offsets - shard_index * pack_rows - dp_index * slot_rows
    )
    target = jnp.where(group_live, base_row[:, None] + positions_in[None, :], pack_rows).reshape(-1)
    layer_weights = (ln_gain, ln_bias, w_qkv, b_qkv, w_o, b_o, w_up, b_up, w_down, b_down)
    image_ids = jnp.arange(counts.shape[0], dtype=jnp.int32)
    packed_rows = dp_index * pack_rows + jnp.arange(pack_rows, dtype=jnp.int32)
    inside = (packed_rows[:, None] >= offsets[None, :]) & (
        packed_rows[:, None] < (offsets + counts)[None, :]
    )
    labels = jnp.max(jnp.where(inside, image_ids[None, :] + 1, 0), axis=1) - 1
    featured = lax.all_to_all(
        tokens.reshape(-1, column_count), "mp", split_axis=1, concat_axis=0, tiled=True
    )
    buffer_rows = (
        jnp.zeros((pack_rows, featured.shape[1]), jnp.bfloat16)
        .at[target]
        .set(featured, mode="drop")
    )
    stream = lax.all_to_all(
        lax.all_to_all(buffer_rows, "dp", split_axis=0, concat_axis=0, tiled=True),
        "mp",
        split_axis=0,
        concat_axis=1,
        tiled=True,
    )
    stream = run_layers(stream, labels, group_rows(shard_count, slot_rows), *layer_weights)
    own_labels = lax.dynamic_slice_in_dim(labels, mp_index * local_rows, local_rows)
    output = jnp.where(own_labels[:, None] >= 0, stream, jnp.zeros_like(stream))
    return output


def solution(mesh):
    in_specs = (
        P(("dp", "mp"), None, None),
        P(),
        P(("dp", "mp"), None),
        P(),
        P(),
        P(),
        P(),
        P(None, None, "dp", "mp"),
        P(None, None, "mp"),
        P(None, "mp", "dp"),
        P(),
        P(None, "dp", "mp"),
        P(None, "mp"),
        P(None, "mp", "dp"),
        P(),
    )
    out_specs = P(("dp", "mp"), None)
    return jax.shard_map(
        per_device, mesh=mesh, in_specs=in_specs, out_specs=out_specs, check_vma=False
    )
```

profile of v0, /device:TPU:0, one launch (start us, length us, event | category | flops | bytes accessed | tf_op | source)
XLA Modules:
  0.0 429.2 jit_solution(11046292865014236250)
XLA Ops:
  8.8 2.1 gather_fusion
  10.9 1.5 copy.54
  12.5 8.7 %gather_fusion.1 = bf16[512,1280]{1,0:T(8,128)(2,1)S(1)} fusion(bf16[8,256,1280]{2,1,0:T(8,128)(2,1)} %param.15, s32[512]{0:T(512)S(1)} %reshape.190), kind=kCustom, calls=%fused_computation.1 | custom fusion | bytes 2625536 | tf_op jit(solution)/shard_map/jit(take_along_axis)/gather | solution.py:115
  21.1 1.5 copy.53
  22.7 3.3 add_convert_fusion.1
  26.0 5.2 %all-to-all-start = ((bf16[512,4,320]{0,2,1:T(8,128)(2,1)}), bf16[512,4,320]{0,2,1:T(8,128)(2,1)S(1)}, u32[]{:S(2)}, u32[]{:S(2)}) async-start(bf16[512,4,320]{0,2,1:T(8,128)(2,1)} %add_convert_fusion.1), calls=%async_computation | async-start | bytes 2621440 | tf_op jit(solution)/shard_map/all_to_all | solution.py:132
  32.2 15.4 %all-to-all-done = bf16[512,4,320]{0,2,1:T(8,128)(2,1)S(1)} async-done(((bf16[512,4,320]{0,2,1:T(8,128)(2,1)}), bf16[512,4,320]{0,2,1:T(8,128)(2,1)S(1)}, u32[]{:S(2)}, u32[]{:S(2)}) %all-to-all-start) | async-done | bytes 1310752 | tf_op jit(solution)/shard_map/all_to_all | solution.py:132
  47.6 1.6 copy.65
  49.2 10.0 %scatter_custom_fusion = bf16[1280,320]{1,0:T(8,128)(2,1)S(1)} fusion(s32[2048]{0:T(1024)S(1)} %bitcast.59, bf16[2048,320]{1,0:T(8,128)(2,1)} %bitcast.57, bf16[]{:T(256)} %constant.58.clone.1), kind=kCustom, calls=%fused_computation.64 | custom fusion | bytes 819712 | tf_op jit(solution)/shard_map/scatter | solution.py:138
  59.2 32.4 %all_to_all.38 = bf16[8,160,320]{2,1,0:T(8,128)(2,1)} all-to-all(bf16[8,160,320]{2,1,0:T(8,128)(2,1)S(1)} %bitcast.55), channel_id=1, replica_groups=mesh['dp'=8,'mp'=4] {'dp'}, dimensions={0} | all-to-all | bytes 1638400 | tf_op jit(solution)/shard_map/all_to_all | solution.py:141
  91.6 3.6 all-to-all-start.2
  95.3 13.2 %all-to-all-done.2 = bf16[4,320,320]{2,1,0:T(8,128)(2,1)S(1)} async-done(((bf16[4,320,320]{2,1,0:T(8,128)(2,1)}), bf16[4,320,320]{2,1,0:T(8,128)(2,1)S(1)}, u32[]{:S(2)}, u32[]{:S(2)}) %all-to-all-start.2) | async-done | bytes 819232 | tf_op jit(solution)/shard_map/all_to_all | solution.py:140
  108.7 2.5 copy.57
  111.2 2.4 reshape.181
  117.6 17.2 %all-gather.1 = bf16[1,320,1280]{1,2,0:T(8,128)(2,1)} all-gather(bf16[1,320,160]{1,2,0:T(8,128)(2,1)S(1)} %copy-done.5), channel_id=3, replica_groups=mesh['dp'=8,'mp'=4] {'dp'}, dimensions={2}, use_global_device_ids=true | all-gather | bytes 921600 | tf_op jit(solution)/shard_map/all_gather | solution.py:33
  134.8 23.6 %all-gather.9.cloned.1.call-done = bf16[1280,1280]{1,0:T(8,128)(2,1)} async-done(((bf16[320,1280]{1,0:T(8,128)(2,1)}), bf16[1280,1280]{1,0:T(8,128)(2,1)}) %all-gather.9.cloned.1.call-update) | async-done | bytes 3276816 | tf_op jit(solution)/shard_map/all_gather | solution.py:19
  158.5 6.2 %fusion.19 = bf16[3,1280,320]{1,2,0:T(8,128)(2,1)S(1)} fusion(bf16[1280,1280]{1,0:T(8,128)(2,1)} %all-gather.9.cloned.1.call-done, bf16[1,3,1280,320]{3,2,1,0:T(8,128)(2,1)} %all-gather.15.cloned.1.call-done, f32[3,320]{1,0:T(4,128)S(1)} %bitcast.60), kind=kOutput, calls=%fused_computation.38 | convolution fusion | flops 3148185600 | bytes 8195840 | tf_op jit(solution)/shard_map/rd,tdc->trc/dot_general | solution.py:23
  166.0 2.8 squeeze.21
  168.8 2.8 squeeze.22
  172.7 10.9 %fusion.49 = (f32[2,4,640]{2,1,0:T(4,128)S(1)}, f32[2,4,640,640]{2,3,1,0:T(8,128)}) fusion(pred[2,640,640]{1,2,0:T(8,128)(4,1)} %broadcast_compare_fusion, bf16[2,640,4,80]{1,0,3,2:T(2,128)(2,1)} %squeeze.22, bf16[2,640,4,80]{1,0,3,2:T(2,128)(2,1)} %squeeze.21), kind=kOutput, calls=%fused_computation.92 | convolution fusion | flops 537395840 | bytes 15585280 | tf_op jit(solution)/shard_map/sub | solution.py:52
  183.7 6.0 %fusion.28 = bf16[2,640,4,80]{1,3,2,0:T(8,128)(2,1)S(1)} fusion(f32[2,4,640,640]{2,3,1,0:T(8,128)} %get-tuple-element.13, f32[2,4,640]{2,1,0:T(4,128)S(1)} %get-tuple-element.12, bf16[2,640,4,80]{1,0,3,2:T(2,128)(2,1)S(1)} %copy-done.4), kind=kOutput, calls=%fused_computation.55 | convolution fusion | flops 531251200 | bytes 14766080 | tf_op jit(solution)/shard_map/bhqk,bkhe->bqhe/dot_general | solution.py:54
  190.8 3.6 convolution_convert_fusion.1
  195.4 44.3 %reduce-scatter.3.cloned.1.call-done = bf16[320,1280]{1,0:T(8,128)(2,1)} async-done(((bf16[1280,1280]{1,0:T(8,128)(2,1)}), bf16[320,1280]{1,0:T(8,128)(2,1)}) %reduce-scatter.3.cloned.1.call-update) | async-done | bytes 819216 | tf_op jit(solution)/shard_map/reduce_scatter | solution.py:35
  239.7 1.5 fusion.47
  241.2 1.6 multiply_reduce_fusion
  244.8 35.7 %all-gather.13.cloned.1.call-done = bf16[1,1280,1280]{2,1,0:T(8,128)(2,1)} async-done(((bf16[1,160,1280]{2,1,0:T(8,128)(2,1)}), bf16[1,1280,1280]{2,1,0:T(8,128)(2,1)}) %all-gather.13.cloned.1.call-update) | async-done | bytes 3276816 | tf_op jit(solution)/shard_map/all_gather | solution.py:26
  280.5 45.5 %all-gather.11.cloned.1.call-done = bf16[1280,1280]{1,0:T(8,128)(2,1)} async-done(((bf16[320,1280]{1,0:T(8,128)(2,1)}), bf16[1280,1280]{1,0:T(8,128)(2,1)}) %all-gather.11.cloned.1.call-update) | async-done | bytes 3276816 | tf_op jit(solution)/shard_map/all_gather | solution.py:19
  326.0 21.0 %fusion.4 = bf16[1280,1280]{1,0:T(8,128)(2,1)} fusion(bf16[1280,1280]{1,0:T(8,128)(2,1)} %all-gather.11.cloned.1.call-done, bf16[1,1280,1280]{2,1,0:T(8,128)(2,1)} %all-gather.13.cloned.1.call-done, f32[1280]{0:T(1024)S(1)} %reduce.9), kind=kOutput, calls=%fused_computation.14 | convolution fusion | flops 4302438400 | bytes 9835520 | tf_op jit(solution)/shard_map/rd,tdc->trc/dot_general | solution.py:23
  347.0 19.9 %all-gather.17.cloned.1.call-done = bf16[1,1280,1280]{1,2,0:T(8,128)(2,1)} async-done(((bf16[1,1280,160]{1,2,0:T(8,128)(2,1)}), bf16[1,1280,1280]{1,2,0:T(8,128)(2,1)}) %all-gather.17.cloned.1.call-update) | async-done | bytes 3276816 | tf_op jit(solution)/shard_map/all_gather | solution.py:33
  366.9 9.1 %convolution_convert_fusion = bf16[1280,1280]{1,0:T(8,128)(2,1)} fusion(bf16[1280,1280]{1,0:T(8,128)(2,1)} %fusion.4, bf16[1,1280,1280]{1,2,0:T(8,128)(2,1)} %all-gather.17.cloned.1.call-done), kind=kOutput, calls=%fused_computation.10 | convolution fusion | flops 4195942400 | bytes 9830400 | tf_op jit(solution)/shard_map/dot_general | solution.py:32
  376.7 43.2 %reduce-scatter.5.cloned.1.call-done = bf16[320,1280]{1,0:T(8,128)(2,1)} async-done(((bf16[1280,1280]{1,0:T(8,128)(2,1)}), bf16[320,1280]{1,0:T(8,128)(2,1)}) %reduce-scatter.5.cloned.1.call-update) | async-done | bytes 819216 | tf_op jit(solution)/shard_map/reduce_scatter | solution.py:35
  419.9 2.4 fusion.30
  (81 shorter events, 14.8 us)
Async XLA Ops:
  6.5 2.2 copy-start
  22.7 9.2 %copy-start.13 = (s32[256]{0:T(256)S(1)}, s32[256]{0:T(256)}, u32[]{:S(2)}) copy-start(s32[256]{0:T(256)} %param.18) | copy-start | bytes 3076
  22.7 9.3 %copy-start.8 = (s32[256]{0:T(256)S(1)}, s32[256]{0:T(256)}, u32[]{:S(2)}) copy-start(s32[256]{0:T(256)} %param.19) | copy-start | bytes 3076
  26.0 21.6 %all-to-all-start = ((bf16[512,4,320]{0,2,1:T(8,128)(2,1)}), bf16[512,4,320]{0,2,1:T(8,128)(2,1)S(1)}, u32[]{:S(2)}, u32[]{:S(2)}) async-start(bf16[512,4,320]{0,2,1:T(8,128)(2,1)} %add_convert_fusion.1), calls=%async_computation | async-start | bytes 2621440 | tf_op jit(solution)/shard_map/all_to_all | solution.py:132
  31.2 103.7 %all-gather.15.cloned.1.call-start = ((), (), s32[]{:S(2)}) async-start(), calls=%async_computation.10 | async-start | bytes 3317760 | tf_op jit(solution)/shard_map/all_gather | solution.py:26
  47.6 47.7 %copy-start.6 = (f32[1,2,1280]{2,1,0:T(2,128)S(1)}, f32[1,2,1280]{2,1,0:T(2,128)}, u32[]{:S(2)}) copy-start(f32[1,2,1280]{2,1,0:T(2,128)} %param.21) | copy-start | bytes 30724
  47.6 47.7 %copy-start.7 = (f32[1,2,1280]{2,1,0:T(2,128)S(1)}, f32[1,2,1280]{2,1,0:T(2,128)}, u32[]{:S(2)}) copy-start(f32[1,2,1280]{2,1,0:T(2,128)} %param.20) | copy-start | bytes 30724
  91.6 16.9 %all-to-all-start.2 = ((bf16[4,320,320]{2,1,0:T(8,128)(2,1)}), bf16[4,320,320]{2,1,0:T(8,128)(2,1)S(1)}, u32[]{:S(2)}, u32[]{:S(2)}) async-start(bf16[4,320,320]{2,1,0:T(8,128)(2,1)} %bitcast.7), calls=%async_computation.2 | async-start | bytes 1966080 | tf_op jit(solution)/shard_map/all_to_all | solution.py:140
  95.3 63.2 %all-gather.9.cloned.1.call-start = ((), (), s32[]{:S(2)}) async-start(), calls=%async_computation.5 | async-start | bytes 4096000 | tf_op jit(solution)/shard_map/all_gather | solution.py:19
  113.6 2.1 copy-start.12
  113.6 4.0 copy-start.5
  115.6 124.1 %reduce-scatter.3.cloned.1.call-start = ((), (), s32[]{:S(2)}) async-start(), calls=%async_computation.6 | async-start | bytes 4096000 | tf_op jit(solution)/shard_map/reduce_scatter | solution.py:35
  172.7 10.9 %copy-start.4 = (bf16[2,640,4,80]{1,0,3,2:T(2,128)(2,1)S(1)}, bf16[2,640,4,80]{1,0,3,2:T(2,128)(2,1)}, u32[]{:S(2)}) copy-start(bf16[2,640,4,80]{1,0,3,2:T(2,128)(2,1)} %squeeze.20) | copy-start | bytes 2457604
  189.6 1.2 copy-start.3
  194.5 0.9 copy-start.9
  194.5 86.0 %all-gather.13.cloned.1.call-start = ((), (), s32[]{:S(2)}) async-start(), calls=%async_computation.8 | async-start | bytes 3686400 | tf_op jit(solution)/shard_map/all_gather | solution.py:26
  195.1 131.0 %all-gather.11.cloned.1.call-start = ((), (), s32[]{:S(2)}) async-start(), calls=%async_computation.7 | async-start | bytes 4096000 | tf_op jit(solution)/shard_map/all_gather | solution.py:19
  239.7 3.1 copy-start.2
  241.2 3.6 copy-start.10
  244.1 122.7 %all-gather.17.cloned.1.call-start = ((), (), s32[]{:S(2)}) async-start(), calls=%async_computation.11 | async-start | bytes 3686400 | tf_op jit(solution)/shard_map/all_gather | solution.py:33
  244.7 175.2 %reduce-scatter.5.cloned.1.call-start = ((), (), s32[]{:S(2)}) async-start(), calls=%async_computation.9 | async-start | bytes 4096000 | tf_op jit(solution)/shard_map/reduce_scatter | solution.py:35
  375.9 0.7 copy-start.11
  375.9 46.5 %copy-start.1 = (bf16[256,1280]{1,0:T(8,128)(2,1)S(1)}, bf16[256,1280]{1,0:T(8,128)(2,1)}, u32[]{:S(2)}) copy-start(bf16[256,1280]{1,0:T(8,128)(2,1)} %param.16) | copy-start | bytes 1966084
Sparse Core Ops, SparseCore 0:
  33.6 40.4 all-gather.14
  115.7 42.7 all-gather.8
  194.6 44.9 reduce-scatter.2
  241.1 39.2 all-gather.12
  282.2 43.8 all-gather.10
  327.5 39.2 all-gather.16
  376.1 43.8 reduce-scatter.4
where the time goes:
time: 430 us; the launch traced here: 429 us
  waiting for transfers between devices  243 us (57%)
  matrix products  56.8 us (13%)
  blocking collectives  49.6 us (12%)
  local copies, waits for them, and re-layouts  40.6 us (9%)
  other arithmetic  16.6 us (4%)
  between operations  13.7 us (3%)
  starting transfers between devices  9.26 us (2%)
    reduce_scatter x2, waiting for transfers between devices, project_sum(): lax.psum_scatter(partials.astype(jnp.bfloat16), 'mp', scatter_dimension=0...  87.5 us
    all_gather x2, waiting for transfers between devices, gather_rows(): return lax.all_gather(normed, 'mp', axis=0, tiled=True)  69.2 us
    all_gather x2, waiting for transfers between devices, fold_rows(): lax.all_gather(weight, 'dp', axis=1, tiled=True)  35.7 us
    all_to_all x1, blocking collectives, per_device(): lax.all_to_all(buffer_rows, 'dp', split_axis=0, concat_axis=0, tiled=True)  32.4 us
    dot_general x2, matrix products, fold_rows(): jnp.einsum('rd,tdc->trc', gathered, lax.all_gather(weight, 'dp', axis=1,...  27.2 us
    all_gather x1, waiting for transfers between devices, project_sum(): lax.all_gather(weight, 'dp', axis=1, tiled=True)  19.9 us
    all_gather x1, blocking collectives, project_sum(): lax.all_gather(weight, 'dp', axis=1, tiled=True)  17.2 us
    all_to_all x1, waiting for transfers between devices, per_device(): lax.all_to_all(tokens.reshape(-1, column_count), 'mp', split_axis=1, conc...  15.4 us
  transfers between devices with their start and end apart: 9, of which 8 were waited for; matrix products, arithmetic and copies ran while one was open for 11% of the time, Pallas kernels for 0%

commit v1 on v0

v1 whole, which is shorter than its diff:
```python
import functools
import math

import jax
import jax.numpy as jnp
from jax import lax
from jax.experimental import pallas as pl
from jax.experimental.pallas import tpu as pltpu
from jax.sharding import PartitionSpec as P

HEAD = 80
MESH = pl.DeviceIdType.MESH


def norm_rows(values, gain_row, shift_row):
    row_mean = jnp.mean(values, axis=-1, keepdims=True)
    centred = values - row_mean
    spread = jnp.mean(centred * centred, axis=-1, keepdims=True)
    return (centred * lax.rsqrt(spread + 1e-06) * gain_row + shift_row).astype(jnp.bfloat16)


def flip(index, mask, count):
    result = index
    bit = 1
    while bit < count:
        wanted = (mask // bit) % 2
        own = (index // bit) % 2
        result = result + bit * wanted * (1 - 2 * own)
        bit = bit * 2
    return result


def tile_of(extent, most):
    tile = most
    while extent % tile != 0:
        tile = tile // 2
    return tile


def route_kernel(shards, groups, packed_ref, out_ref, send_sem, recv_sem, own_sem):
    per = shards // groups
    dp = lax.axis_index("dp")
    mp = lax.axis_index("mp")
    home = dp // per
    slot = lax.rem(dp, per) * groups + mp

    barrier = pltpu.get_barrier_semaphore()
    for j in range(per):
        for g in range(groups):
            source = mp * per + j

            @pl.when(jnp.logical_or(source != dp, mp != g))
            def _():
                pl.semaphore_signal(barrier, inc=1, device_id=(source, g), device_id_type=MESH)

    is_home = home == mp

    @pl.when(is_home)
    def _():
        pl.semaphore_wait(barrier, shards - 1)

    @pl.when(jnp.logical_not(is_home))
    def _():
        pl.semaphore_wait(barrier, shards)

    def remote(step):
        dest = lax.rem(dp + step, shards)
        return pltpu.make_async_remote_copy(
            src_ref=packed_ref.at[dest],
            dst_ref=out_ref.at[slot],
            send_sem=send_sem.at[step],
            recv_sem=recv_sem.at[slot],
            device_id=(dest, home),
            device_id_type=MESH,
        )

    own = pltpu.make_async_copy(packed_ref.at[dp], out_ref.at[slot], own_sem)
    for step in range(1, shards):
        remote(step).start()

    @pl.when(is_home)
    def _():
        own.start()
        own.wait()

    @pl.when(jnp.logical_not(is_home))
    def _():
        remote(0).start()
        remote(0).wait_send()

    for step in range(1, shards):
        remote(step).wait_send()
    for j in range(per):
        for g in range(groups):
            source = mp * per + j

            @pl.when(jnp.logical_or(source != dp, mp != g))
            def _():
                pltpu.make_async_remote_copy(
                    src_ref=packed_ref.at[0],
                    dst_ref=out_ref.at[j * groups + g],
                    send_sem=send_sem.at[0],
                    recv_sem=recv_sem.at[j * groups + g],
                    device_id=(dp, mp),
                    device_id_type=MESH,
                ).wait_recv()


def route(packed, shards, groups):
    vmem = pl.BlockSpec(memory_space=pltpu.VMEM)
    return pl.pallas_call(
        functools.partial(route_kernel, shards, groups),
        out_shape=jax.ShapeDtypeStruct(packed.shape, packed.dtype),
        in_specs=[vmem],
        out_specs=vmem,
        scratch_shapes=[
            pltpu.SemaphoreType.DMA((shards,)),
            pltpu.SemaphoreType.DMA((shards,)),
            pltpu.SemaphoreType.DMA,
        ],
        compiler_params=pltpu.CompilerParams(collective_id=0, has_side_effects=True),
        cost_estimate=pl.CostEstimate(flops=15_000_000_000, bytes_accessed=0, transcendentals=0),
        name="route",
    )(packed)


def exchange(groups, x_ref, blocks, parts, backs, sems, block_step, finish):
    own_sem, send_a, recv_a, send_b, recv_b = sems
    dp = lax.axis_index("dp")
    mp = lax.axis_index("mp")

    barrier = pltpu.get_barrier_semaphore()
    for k in range(1, groups):
        pl.semaphore_signal(
            barrier, inc=1, device_id=(dp, flip(mp, k, groups)), device_id_type=MESH
        )
    own = pltpu.make_async_copy(x_ref, blocks.at[0], own_sem)
    own.start()
    pl.semaphore_wait(barrier, groups - 1)

    def out_copy(k):
        return pltpu.make_async_remote_copy(
            src_ref=x_ref,
            dst_ref=blocks.at[k],
            send_sem=send_a.at[k],
            recv_sem=recv_a.at[k],
            device_id=(dp, flip(mp, k, groups)),
            device_id_type=MESH,
        )

    def back_copy(k):
        return pltpu.make_async_remote_copy(
            src_ref=parts.at[k],
            dst_ref=backs.at[k],
            send_sem=send_b.at[k],
            recv_sem=recv_b.at[k],
            device_id=(dp, flip(mp, k, groups)),
            device_id_type=MESH,
        )

    for k in range(1, groups):
        out_copy(k).start()
    own.wait()

    def step(k, carry):
        @pl.when(k > 0)
        def _():
            out_copy(k).wait_recv()

        block_step(k, flip(mp, k, groups))

        @pl.when(k > 0)
        def _():
            back_copy(k).start()

        return carry

    lax.fori_loop(0, groups, step, 0)
    for k in range(1, groups):
        back_copy(k).wait_recv()
    finish()
    for k in range(1, groups):
        out_copy(k).wait_send()
        back_copy(k).wait_send()


def sum_parts(groups, parts, backs, rows):
    total = parts[0, rows, :].astype(jnp.float32)
    for k in range(1, groups):
        total = total + backs[k, rows, :].astype(jnp.float32)
    return total


def attention_kernel(
    groups,
    x_ref,
    stream_ref,
    w_ref,
    b_ref,
    label_col_ref,
    label_row_ref,
    bias_ref,
    gain_ref,
    shift_ref,
    residual_ref,
    normed_ref,
    blocks,
    parts,
    backs,
    attended_ref,
    *sems,
):
    row_count, depth = x_ref.shape
    width = w_ref.shape[2]
    heads = width // HEAD
    scale = 1.0 / math.sqrt(HEAD)
    tile = tile_of(depth, 256)

    def block_step(k, source):
        x = blocks[k]

        def project(t):
            y = jnp.dot(x, w_ref[t], preferred_element_type=jnp.float32)
            return (y + b_ref[t]).astype(jnp.bfloat16)

        query, key, value = project(0), project(1), project(2)
        matches = label_col_ref[source] == label_row_ref[source]
        lane_head = lax.broadcasted_iota(jnp.int32, (row_count, width), 1)
        total = jnp.zeros((row_count, width), jnp.float32)
        zero = jnp.zeros((row_count, width), jnp.bfloat16)
        for h in range(heads):
            inside = (lane_head >= h * HEAD) & (lane_head < (h + 1) * HEAD)
            scores = lax.dot_general(
                jnp.where(inside, query, zero),
                key,
                (((1,), (1,)), ((), ())),
                preferred_element_type=jnp.float32,
            )
            scores = jnp.where(matches, scores * scale, -jnp.inf)
            weights = jnp.exp(scores - jnp.max(scores, axis=-1, keepdims=True))
            inverse = 1.0 / jnp.sum(weights, axis=-1, keepdims=True)
            probabilities = (weights * inverse).astype(jnp.bfloat16)
            total = total + jnp.dot(
                probabilities, jnp.where(inside, value, zero), preferred_element_type=jnp.float32
            )
        attended_ref[...] = total.astype(jnp.bfloat16)

        def column(t, carry):
            at = pl.ds(pl.multiple_of(t * tile, tile), tile)
            parts[k, :, at] = lax.dot_general(
                attended_ref[...],
                w_ref[3, at, :],
                (((1,), (1,)), ((), ())),
                preferred_element_type=jnp.float32,
            ).astype(jnp.bfloat16)
            return carry

        lax.fori_loop(0, depth // tile, column, 0)

    def finish():
        rows_tile = tile_of(row_count, 32)

        def some(i, carry):
            rows = pl.ds(pl.multiple_of(i * rows_tile, rows_tile), rows_tile)
            residual = (
                stream_ref[rows, :].astype(jnp.float32)
                + sum_parts(groups, parts, backs, rows)
                + bias_ref[...]
            )
            residual_ref[rows, :] = residual
            normed_ref[rows, :] = norm_rows(residual, gain_ref[...], shift_ref[...])
            return carry

        lax.fori_loop(0, row_count // rows_tile, some, 0)

    exchange(groups, x_ref, blocks, parts, backs, sems, block_step, finish)


def mlp_kernel(
    groups,
    x_ref,
    residual_ref,
    up_ref,
    b_ref,
    down_ref,
    bias_ref,
    out_ref,
    blocks,
    parts,
    backs,
    hidden_ref,
    *sems,
):
    row_count, depth = x_ref.shape
    width = up_ref.shape[1]
    tile = tile_of(depth, 256)
    up_tile = tile_of(width, 256)

    def block_step(k, source):
        def up(t, carry):
            at = pl.ds(pl.multiple_of(t * up_tile, up_tile), up_tile)
            y = jnp.dot(blocks[k], up_ref[:, at], preferred_element_type=jnp.float32) + b_ref[:, at]
            y = 0.5 * y * (1.0 + lax.erf(y * math.sqrt(0.5)))
            hidden_ref[:, at] = y.astype(jnp.bfloat16)
            return carry

        lax.fori_loop(0, width // up_tile, up, 0)

        def column(t, carry):
            at = pl.ds(pl.multiple_of(t * tile, tile), tile)
            parts[k, :, at] = jnp.dot(
                hidden_ref[...], down_ref[:, at], preferred_element_type=jnp.float32
            ).astype(jnp.bfloat16)
            return carry

        lax.fori_loop(0, depth // tile, column, 0)

    def finish():
        rows_tile = tile_of(row_count, 32)

        def some(i, carry):
            rows = pl.ds(pl.multiple_of(i * rows_tile, rows_tile), rows_tile)
            out_ref[rows, :] = (
                residual_ref[rows, :] + sum_parts(groups, parts, backs, rows) + bias_ref[...]
            ).astype(jnp.bfloat16)
            return carry

        lax.fori_loop(0, row_count // rows_tile, some, 0)

    exchange(groups, x_ref, blocks, parts, backs, sems, block_step, finish)


def exchange_call(kernel, groups, args, outs, width, collective_id, name):
    row_count, depth = args[0].shape
    vmem = pl.BlockSpec(memory_space=pltpu.VMEM)
    many = pltpu.SemaphoreType.DMA((groups,))
    return pl.pallas_call(
        functools.partial(kernel, groups),
        out_shape=outs,
        in_specs=[vmem] * len(args),
        out_specs=jax.tree.map(lambda _: vmem, outs),
        scratch_shapes=[
            pltpu.VMEM((groups, row_count, depth), jnp.bfloat16),
            pltpu.VMEM((groups, row_count, depth), jnp.bfloat16),
            pltpu.VMEM((groups, row_count, depth), jnp.bfloat16),
            pltpu.VMEM((row_count, width), jnp.bfloat16),
            pltpu.SemaphoreType.DMA,
            many,
            many,
            many,
            many,
        ],
        compiler_params=pltpu.CompilerParams(
            collective_id=collective_id, has_side_effects=True, vmem_limit_bytes=48 * 1024 * 1024
        ),
        cost_estimate=pl.CostEstimate(flops=50_000_000_000, bytes_accessed=0, transcendentals=0),
        name=name,
    )(*args)


def per_device(
    patches,
    position,
    keep,
    counts,
    offsets,
    ln_gain,
    ln_bias,
    w_qkv,
    b_qkv,
    w_o,
    b_o,
    w_up,
    b_up,
    w_down,
    b_down,
):
    local_images, patch_count, column_count = patches.shape
    keep_most = keep.shape[1]
    shard_count = lax.axis_size("dp")
    group_size = lax.axis_size("mp")
    images_here = local_images * group_size
    per_slot = (images_here + shard_count - 1) // shard_count
    slot_rows = max(keep_most + 16, per_slot * keep_most * 5 // 8)
    pack_rows = slot_rows * shard_count
    local_rows = pack_rows // group_size
    dp_index = lax.axis_index("dp")
    mp_index = lax.axis_index("mp")
    f32 = jnp.float32

    attention_shard = jnp.concatenate([w_qkv[0], w_o[0].T[None]], axis=0)
    w_attention = lax.all_gather(attention_shard, "dp", axis=1, tiled=True)
    w_up_full = lax.all_gather(w_up[0], "dp", axis=0, tiled=True)
    w_down_full = lax.all_gather(w_down[0], "dp", axis=1, tiled=True)

    chosen = (keep[:, :, None] == jnp.arange(patch_count, dtype=jnp.int32)).astype(jnp.bfloat16)
    tokens = (
        jnp.einsum("ijp,ipd->ijd", chosen, patches, preferred_element_type=f32)
        + jnp.einsum("ijp,pd->ijd", chosen, position, preferred_element_type=f32)
    ).astype(jnp.bfloat16)

    first_image = dp_index * images_here
    group_counts = lax.dynamic_slice_in_dim(counts, first_image, images_here)
    group_offsets = lax.dynamic_slice_in_dim(offsets, first_image, images_here)
    positions_in = jnp.arange(keep_most, dtype=jnp.int32)
    group_live = positions_in[None, :] < group_counts[:, None]
    shard_index = group_offsets // pack_rows
    base_row = (
        shard_index * slot_rows + group_offsets - shard_index * pack_rows - dp_index * slot_rows
    )
    target = jnp.where(group_live, base_row[:, None] + positions_in[None, :], pack_rows).reshape(-1)
    image_ids = jnp.arange(counts.shape[0], dtype=jnp.int32)
    packed_rows = dp_index * pack_rows + jnp.arange(pack_rows, dtype=jnp.int32)
    inside = (packed_rows[:, None] >= offsets[None, :]) & (
        packed_rows[:, None] < (offsets + counts)[None, :]
    )
    labels = jnp.max(jnp.where(inside, image_ids[None, :] + 1, 0), axis=1) - 1

    featured = lax.all_to_all(
        tokens.reshape(-1, column_count), "mp", split_axis=1, concat_axis=0, tiled=True
    )
    feature_count = featured.shape[1]
    placing = (jnp.arange(pack_rows, dtype=jnp.int32)[:, None] == target[None, :]).astype(
        jnp.bfloat16
    )
    packed = jnp.dot(placing, featured, preferred_element_type=f32).astype(jnp.bfloat16)
    arrived = route(
        packed.reshape(shard_count, slot_rows, feature_count), shard_count, group_size
    )
    per = shard_count // group_size
    stream = (
        arrived.reshape(per, group_size, slot_rows, feature_count)
        .transpose(0, 2, 1, 3)
        .reshape(local_rows, column_count)
    )
    normed = norm_rows(stream.astype(f32), ln_gain[0, 0], ln_bias[0, 0])
    by_group = labels.reshape(group_size, local_rows)
    residual, normed_mlp = exchange_call(
        attention_kernel,
        group_size,
        (
            normed,
            stream,
            w_attention,
            b_qkv[0][:, None, :],
            by_group[:, :, None],
            by_group[:, None, :],
            b_o,
            ln_gain[:, 1],
            ln_bias[:, 1],
        ),
        (
            jax.ShapeDtypeStruct((local_rows, column_count), f32),
            jax.ShapeDtypeStruct((local_rows, column_count), jnp.bfloat16),
        ),
        w_attention.shape[2],
        1,
        "attention",
    )
    stream = exchange_call(
        mlp_kernel,
        group_size,
        (normed_mlp, residual, w_up_full, b_up, w_down_full, b_down),
        jax.ShapeDtypeStruct((local_rows, column_count), jnp.bfloat16),
        w_up_full.shape[1],
        2,
        "mlp",
    )
    own_labels = lax.dynamic_slice_in_dim(labels, mp_index * local_rows, local_rows)
    return jnp.where(own_labels[:, None] >= 0, stream, jnp.zeros_like(stream))


def solution(mesh):
    in_specs = (
        P(("dp", "mp"), None, None),
        P(),
        P(("dp", "mp"), None),
        P(),
        P(),
        P(),
        P(),
        P(None, None, "dp", "mp"),
        P(None, None, "mp"),
        P(None, "mp", "dp"),
        P(),
        P(None, "dp", "mp"),
        P(None, "mp"),
        P(None, "mp", "dp"),
        P(),
    )
    out_specs = P(("dp", "mp"), None)
    return jax.shard_map(
        per_device, mesh=mesh, in_specs=in_specs, out_specs=out_specs, check_vma=False
    )
```

time: 430 us -> 275 us (0.64)
  waiting for transfers between devices: 243 us -> 36.9 us
  Pallas kernels: 0 us -> 182 us
  matrix products: 56.8 us -> 6.31 us
  blocking collectives: 49.6 us -> 0 us
  local copies, waits for them, and re-layouts: 40.6 us -> 20.5 us
  other arithmetic: 16.6 us -> 10.2 us
    pallas_call x0 -> x3, Pallas kernels: none -> 182 us  [the longest x2 157 us: exchange_call(): pl.pallas_call(functools.partial(kernel, groups), out_shape=outs, in_spec...]
    all_gather x5 -> x3, waiting for transfers between devices: 125 us -> 21.3 us  [the longest x1 21.2 us: per_device(): w_attention = lax.all_gather(attention_shard, 'dp', axis=1, tiled=True)]
    reduce_scatter x2 -> x0, waiting for transfers between devices: 87.5 us -> none  [project_sum(): lax.psum_scatter(partials.astype(jnp.bfloat16), 'mp', scatter_dimension=0...]
    dot_general x5 -> x3, matrix products: 45.8 us -> 6.31 us  [the longest x1 3.56 us: per_device(): jnp.einsum('ijp,ipd->ijd', chosen, patches, preferred_element_type=f32)]
    all_to_all x1 -> x0, blocking collectives: 32.4 us -> none  [per_device(): lax.all_to_all(buffer_rows, 'dp', split_axis=0, concat_axis=0, tiled=True)]
    all_gather x1 -> x0, blocking collectives: 17.2 us -> none  [project_sum(): lax.all_gather(weight, 'dp', axis=1, tiled=True)]
    gather x5 -> x0, local copies, waits for them, and re-layouts: 13.8 us -> none  [the longest x3 10.2 us: per_device(): picked = jnp.take_along_axis(patches, keep[:, :, None], axis=1)]
    all_to_all x1 -> x0, waiting for transfers between devices: 13.2 us -> none  [per_device(): lax.all_to_all(lax.all_to_all(buffer_rows, 'dp', split_axis=0, concat_axi...]
  transfers between devices with their start and end apart: 9 -> 4, of which waited for: 8 -> 2; matrix products, arithmetic and copies ran while one was open for 11% -> 11% of each run, Pallas kernels for 0% -> 38%
where the time goes in v1:
time: 275 us
  Pallas kernels  182 us (66%)
  waiting for transfers between devices  36.9 us (13%)
  local copies, waits for them, and re-layouts  20.5 us (7%)
  between operations  13.3 us (5%)
  other arithmetic  10.2 us (4%)
  matrix products  6.31 us (2%)
  starting transfers between devices  5.38 us (2%)
    pallas_call x2, Pallas kernels, exchange_call(): pl.pallas_call(functools.partial(kernel, groups), out_shape=outs, in_spec...  157 us
    pallas_call x1, Pallas kernels, route(): pl.pallas_call(functools.partial(route_kernel, shards, groups), out_shape...  25.7 us
    all_gather x1, waiting for transfers between devices, per_device(): w_attention = lax.all_gather(attention_shard, 'dp', axis=1, tiled=True)  21.2 us
    all_to_all x1, waiting for transfers between devices, per_device(): lax.all_to_all(tokens.reshape(-1, column_count), 'mp', split_axis=1, conc...  14.2 us
    all_gather x1, local copies, waits for them, and re-layouts, per_device(): w_down_full = lax.all_gather(w_down[0], 'dp', axis=1, tiled=True)  5.68 us
  transfers between devices with their start and end apart: 4, of which 2 were waited for; matrix products, arithmetic and copies ran while one was open for 11% of the time, Pallas kernels for 38%

profile of v1, /device:TPU:0, one launch (start us, length us, event | category | flops | bytes accessed | tf_op | source)
XLA Modules:
  0.0 274.8 jit_solution(7891143209198851309)
XLA Ops:
  6.5 0.7 all-gather.10.cloned.1.call-update
  7.3 1.9 pad_maximum_fusion
  9.3 3.6 %fusion.7 = f32[8,64,1280]{2,1,0:T(8,128)S(1)} fusion(bf16[8,256,1280]{2,1,0:T(8,128)(2,1)} %param.15, s32[8,64]{1,0:T(8,128)S(1)} %copy-done.10), kind=kOutput, calls=%fused_computation.16 | convolution fusion | flops 335675392 | bytes 7866368 | tf_op jit(solution)/shard_map/ijp,ipd->ijd/dot_general | solution.py:398
  12.8 0.6 fusion.2
  13.4 1.8 all_to_all.14
  15.2 2.5 copy.30
  17.7 5.3 %all-to-all-start = ((bf16[512,4,320]{0,2,1:T(8,128)(2,1)}), bf16[512,4,320]{0,2,1:T(8,128)(2,1)S(1)}, u32[]{:S(2)}, u32[]{:S(2)}) async-start(bf16[512,4,320]{0,2,1:T(8,128)(2,1)} %copy.30), calls=%async_computation | async-start | bytes 2621440 | tf_op jit(solution)/shard_map/all_to_all | solution.py:419
  23.0 0.7 all-gather.8.cloned.1.call-update
  23.8 0.5 select_reduce_fusion
  24.2 0.5 sub.47.label_col_ref
  24.9 0.1 subtract_subtract_fusion
  25.2 14.2 %all-to-all-done = bf16[512,4,320]{0,2,1:T(8,128)(2,1)S(1)} async-done(((bf16[512,4,320]{0,2,1:T(8,128)(2,1)}), bf16[512,4,320]{0,2,1:T(8,128)(2,1)S(1)}, u32[]{:S(2)}, u32[]{:S(2)}) %all-to-all-start) | async-done | bytes 1310752 | tf_op jit(solution)/shard_map/all_to_all | solution.py:419
  39.4 0.1 copy.36
  39.6 2.2 fusion.3
  41.8 1.3 copy.32
  43.1 25.7 %route.1 = bf16[8,160,320]{2,1,0:T(8,128)(2,1)} custom-call(bf16[8,160,320]{2,1,0:T(8,128)(2,1)} %bitcast.38), custom_call_target="tpu_custom_call" | custom-call | flops 15000000512 | tf_op jit(solution)/shard_map/route/pallas_call | solution.py:111
  68.8 2.4 convert_reduce_fusion
  71.2 1.5 copy.42
  72.7 0.1 div.16
  72.8 3.7 %fusion.5 = f32[2,160]{1,0:T(2,128)S(1)} fusion(f32[2,160]{1,0:T(2,128)S(1)} %broadcast_multiply_fusion, bf16[2,4,160,320]{3,2,1,0:T(8,128)(2,1)S(1)} %bitcast.33), kind=kLoop, calls=%fused_computation.9 | loop fusion | flops 1638080 | bytes 821760 | tf_op jit(solution)/shard_map/reduce_sum | solution.py:18
  76.5 0.1 rsqrt.12
  76.6 2.1 reshape.121.stream_ref
  78.6 0.4 add_convert_fusion.x_ref
  79.1 5.7 %copy.35 = bf16[1,1280,1280]{2,1,0:T(8,128)(2,1)} copy(bf16[1,1280,1280]{1,2,0:T(8,128)(2,1)} %all-gather.10.cloned.1.call-done) | data formatting | bytes 6553600 | tf_op jit(solution)/shard_map/all_gather | solution.py:394
  84.7 21.2 %all-gather.6.cloned.1.call-done.w_ref = bf16[4,1280,320]{2,1,0:T(8,128)(2,1)} async-done(((bf16[4,160,320]{2,1,0:T(8,128)(2,1)}), bf16[4,1280,320]{2,1,0:T(8,128)(2,1)}) %all-gather.6.cloned.1.call-update) | async-done | bytes 3276816 | tf_op jit(solution)/shard_map/all_gather | solution.py:392
  106.0 79.8 %attention.1 = (f32[320,1280]{1,0:T(8,128)S(1)}, bf16[320,1280]{1,0:T(8,128)(2,1)S(1)}) custom-call(bf16[320,1280]{1,0:T(8,128)(2,1)S(1)} %add_convert_fusion.x_ref, bf16[320,1280]{1,0:T(8,128)(2,1)S(1)} %reshape.121.stream_ref, bf16[4,1280,320]{2,1,0:T(8,128)(2,1)} %all-gather.6.cloned.1.call-done.w_ref, f32[3,1,320]{2,1,0:T(1,128)S(1)} %bitcast.30, ...), custom_call_target="tpu_custom_call" | custom-call | flops 49999998976 | tf_op jit(solution)/shard_map/attention/pallas_call | solution.py:337
  185.8 1.3 copy-done.5
  187.0 0.9 copy-done.7
  187.9 1.4 copy-done.6
  189.4 1.1 copy-done.8
  190.5 76.8 %mlp.1 = bf16[320,1280]{1,0:T(8,128)(2,1)S(1)} custom-call(bf16[320,1280]{1,0:T(8,128)(2,1)S(1)} %copy-done.8, f32[320,1280]{1,0:T(8,128)S(1)} %copy-done.6, bf16[1280,1280]{1,0:T(8,128)(2,1)} %bitcast.41, f32[1,1280]{1,0:T(1,128)S(1)} %copy-done.2, bf16[1280,1280]{1,0:T(8,128)(2,1)} %bitcast.36, f32[1,1280]{1,0:T(1,128)S(1)} %copy-done.3), custom_call_target="tpu_custom_call" | custom-call | flops 49999998976 | tf_op jit(solution)/shard_map/mlp/pallas_call | solution.py:337
  267.3 1.0 broadcast_select_fusion
  (44 shorter events, 0.6 us)
Async XLA Ops:
  6.5 6.3 %copy-start = (bf16[256,1280]{1,0:T(8,128)(2,1)S(1)}, bf16[256,1280]{1,0:T(8,128)(2,1)}, u32[]{:S(2)}) copy-start(bf16[256,1280]{1,0:T(8,128)(2,1)} %param.16) | copy-start | bytes 1966084
  6.5 2.7 copy-start.10
  6.5 72.5 %all-gather.10.cloned.1.call-start = ((), (), s32[]{:S(2)}) async-start(), calls=%async_computation.3 | async-start | bytes 3686400 | tf_op jit(solution)/shard_map/all_gather | solution.py:394
  7.3 98.7 %all-gather.6.cloned.1.call-start = ((), (), s32[]{:S(2)}) async-start(), calls=%async_computation.1 | async-start | bytes 4423680 | tf_op jit(solution)/shard_map/all_gather | solution.py:392
  17.6 6.1 %copy-start.13 = (s32[256]{0:T(256)S(1)}, s32[256]{0:T(256)}, u32[]{:S(2)}) copy-start(s32[256]{0:T(256)} %param.19) | copy-start | bytes 3076
  17.6 6.1 %copy-start.14 = (s32[256]{0:T(256)S(1)}, s32[256]{0:T(256)}, u32[]{:S(2)}) copy-start(s32[256]{0:T(256)} %param.18) | copy-start | bytes 3076
  17.6 7.6 %copy-start.11 = (f32[1,2,1280]{2,1,0:T(2,128)S(1)}, f32[1,2,1280]{2,1,0:T(2,128)}, u32[]{:S(2)}) copy-start(f32[1,2,1280]{2,1,0:T(2,128)} %param.21) | copy-start | bytes 30724
  17.7 7.6 %copy-start.12 = (f32[1,2,1280]{2,1,0:T(2,128)S(1)}, f32[1,2,1280]{2,1,0:T(2,128)}, u32[]{:S(2)}) copy-start(f32[1,2,1280]{2,1,0:T(2,128)} %param.20) | copy-start | bytes 30724
  17.7 21.8 %all-to-all-start = ((bf16[512,4,320]{0,2,1:T(8,128)(2,1)}), bf16[512,4,320]{0,2,1:T(8,128)(2,1)S(1)}, u32[]{:S(2)}, u32[]{:S(2)}) async-start(bf16[512,4,320]{0,2,1:T(8,128)(2,1)} %copy.30), calls=%async_computation | async-start | bytes 2621440 | tf_op jit(solution)/shard_map/all_to_all | solution.py:419
  23.0 164.9 %all-gather.8.cloned.1.call-start = ((), (), s32[]{:S(2)}) async-start(), calls=%async_computation.2 | async-start | bytes 3686400 | tf_op jit(solution)/shard_map/all_gather | solution.py:393
  68.8 2.5 copy-start.9
  79.0 27.0 %copy-start.1 = (f32[1,1280]{1,0:T(1,128)S(1)}, f32[1,1280]{1,0:T(1,128)}, u32[]{:S(2)}) copy-start(f32[1,1280]{1,0:T(1,128)} %bias_ref.2) | copy-start | bytes 15364
  79.0 27.0 %copy-start.4 = (f32[1,3,320]{2,0,1:T(1,128)S(1)}, f32[1,3,320]{2,0,1:T(1,128)}, u32[]{:S(2)}) copy-start(f32[1,3,320]{2,0,1:T(1,128)} %param.23) | copy-start | bytes 11524
  106.0 82.0 %copy-start.2 = (f32[1,1280]{1,0:T(1,128)S(1)}, f32[1,1280]{1,0:T(1,128)}, u32[]{:S(2)}) copy-start(f32[1,1280]{1,0:T(1,128)} %b_ref.1) | copy-start | bytes 15364
  106.0 82.0 %copy-start.3 = (f32[1,1280]{1,0:T(1,128)S(1)}, f32[1,1280]{1,0:T(1,128)}, u32[]{:S(2)}) copy-start(f32[1,1280]{1,0:T(1,128)} %bias_ref.3) | copy-start | bytes 15364
  185.8 1.3 copy-start.5
  187.0 0.9 copy-start.7
  187.9 1.4 copy-start.6
  189.4 1.1 copy-start.8
Sparse Core Ops, SparseCore 0:
  9.0 42.0 all-gather.9
  52.6 53.2 all-gather.5
  107.6 40.4 all-gather.7

commit v2 on v1

--- a/solution.py
+++ b/solution.py
@@ -37,7 +37,19 @@
     return tile
 
 
-def route_kernel(shards, groups, packed_ref, out_ref, send_sem, recv_sem, own_sem):
+def route_kernel(
+    shards,
+    groups,
+    packed_ref,
+    gain_ref,
+    shift_ref,
+    stream_ref,
+    normed_ref,
+    out_ref,
+    send_sem,
+    recv_sem,
+    own_sem,
+):
     per = shards // groups
     dp = lax.axis_index("dp")
     mp = lax.axis_index("mp")
@@ -105,15 +117,34 @@
                     device_id_type=MESH,
                 ).wait_recv()
 
-
-def route(packed, shards, groups):
+    rows_tile = tile_of(packed_ref.shape[1], 32)
+    for j in range(per):
+
+        def some(i, carry):
+            rows = pl.ds(pl.multiple_of(i * rows_tile, rows_tile), rows_tile)
+            whole = jnp.concatenate(
+                [out_ref[j * groups + g, rows, :] for g in range(groups)], axis=-1
+            )
+            stream_ref[j, rows, :] = whole
+            normed_ref[j, rows, :] = norm_rows(
+                whole.astype(jnp.float32), gain_ref[...], shift_ref[...]
+            )
+            return carry
+
+        lax.fori_loop(0, packed_ref.shape[1] // rows_tile, some, 0)
+
+
+def route(packed, gain_row, shift_row, shards, groups):
+    slot_rows, width = packed.shape[1:]
+    result = jax.ShapeDtypeStruct((shards // groups, slot_rows, width * groups), packed.dtype)
     vmem = pl.BlockSpec(memory_space=pltpu.VMEM)
     return pl.pallas_call(
         functools.partial(route_kernel, shards, groups),
-        out_shape=jax.ShapeDtypeStruct(packed.shape, packed.dtype),
-        in_specs=[vmem],
-        out_specs=vmem,
+        out_shape=(result, result),
+        in_specs=[vmem] * 3,
+        out_specs=(vmem, vmem),
         scratch_shapes=[
+            pltpu.VMEM(packed.shape, packed.dtype),
             pltpu.SemaphoreType.DMA((shards,)),
             pltpu.SemaphoreType.DMA((shards,)),
             pltpu.SemaphoreType.DMA,
@@ -121,74 +152,167 @@
         compiler_params=pltpu.CompilerParams(collective_id=0, has_side_effects=True),
         cost_estimate=pl.CostEstimate(flops=15_000_000_000, bytes_accessed=0, transcendentals=0),
         name="route",
-    )(packed)
-
-
-def exchange(groups, x_ref, blocks, parts, backs, sems, block_step, finish):
+    )(packed, gain_row, shift_row)
+
+
+def exchange(groups, x_ref, blocks, parts, backs, relay, sems, block_step, finish):
     own_sem, send_a, recv_a, send_b, recv_b = sems
     dp = lax.axis_index("dp")
     mp = lax.axis_index("mp")
+    pieces = x_ref.shape[0]
+    square = groups == 4 and pieces == 2
+    partners = range(1, 3) if square else range(1, groups)
 
     barrier = pltpu.get_barrier_semaphore()
-    for k in range(1, groups):
+    for k in partners:
         pl.semaphore_signal(
             barrier, inc=1, device_id=(dp, flip(mp, k, groups)), device_id_type=MESH
         )
-    own = pltpu.make_async_copy(x_ref, blocks.at[0], own_sem)
+    own = pltpu.make_async_copy(x_ref, blocks.at[pl.ds(0, pieces)], own_sem)
     own.start()
-    pl.semaphore_wait(barrier, groups - 1)
-
-    def out_copy(k):
+    pl.semaphore_wait(barrier, len(partners))
+
+    def send(source, target, out_sem, in_sem, k):
         return pltpu.make_async_remote_copy(
-            src_ref=x_ref,
-            dst_ref=blocks.at[k],
-            send_sem=send_a.at[k],
-            recv_sem=recv_a.at[k],
+            src_ref=source,
+            dst_ref=target,
+            send_sem=out_sem,
+            recv_sem=in_sem,
             device_id=(dp, flip(mp, k, groups)),
             device_id_type=MESH,
         )
 
-    def back_copy(k):
-        return pltpu.make_async_remote_copy(
-            src_ref=parts.at[k],
-            dst_ref=backs.at[k],
-            send_sem=send_b.at[k],
-            recv_sem=recv_b.at[k],
-            device_id=(dp, flip(mp, k, groups)),
-            device_id_type=MESH,
-        )
-
-    for k in range(1, groups):
-        out_copy(k).start()
+    def out_copy(k, h):
+        at = k * pieces + h
+        return send(x_ref.at[h], blocks.at[at], send_a.at[at], recv_a.at[at], k)
+
+    def back_copy(k, h):
+        at = k * pieces + h
+        return send(parts.at[at], backs.at[at], send_b.at[at], recv_b.at[at], k)
+
+    if square:
+        def forward(h):
+            held, k = (2, 2) if h == 0 else (5, 1)
+            at = 6 + h
+            return send(blocks.at[held], blocks.at[at], send_a.at[at], recv_a.at[at], k)
+
+        def across(h):
+            at = 6 + h
+            return send(parts.at[at], relay.at[h], send_b.at[at], recv_b.at[at], 1 + h)
+
+        for k, h in ((1, 0), (2, 1), (1, 1), (2, 0)):
+            out_copy(k, h).start()
+        own.wait()
+
+        def step(i, carry):
+            late = (i + 2) // 8
+            middle = ((i + 2) // 4) % 2
+            k = middle * (1 + i % 2) + 3 * late
+            h = (i // 4 + i % 2) % 2
+
+            @pl.when(i == 2)
+            def _():
+                out_copy(1, 0).wait_recv()
+                forward(0).start()
+                out_copy(2, 1).wait_recv()
+                forward(1).start()
+
+            @pl.when(i >= 4)
+            def _():
+                out_copy(k, h).wait_recv()
+
+            block_step(k * 2 + h, flip(mp, k, groups) * 2 + h)
+
+            @pl.when(i == 2)
+            def _():
+                back_copy(1, 0).start()
+
+            @pl.when(i == 3)
+            def _():
+                back_copy(2, 1).start()
+
+            @pl.when(i == 6)
+            def _():
+                across(1).start()
+
+            @pl.when(i == 7)
+            def _():
+                across(0).start()
+
+            return carry
+
+        lax.fori_loop(0, 8, step, 0)
+        rows_tile = tile_of(x_ref.shape[1], 32)
+        for h, k in ((1, 1), (0, 2)):
+            across(h).wait_recv()
+
+            def add(i, carry, h=h, k=k):
+                rows = pl.ds(pl.multiple_of(i * rows_tile, rows_tile), rows_tile)
+                parts[k * 2 + h, rows, :] = (
+                    parts[k * 2 + h, rows, :].astype(jnp.float32)
+                    + relay[h, rows, :].astype(jnp.float32)
+                ).astype(jnp.bfloat16)
+                return carry
+
+            lax.fori_loop(0, x_ref.shape[1] // rows_tile, add, 0)
+            back_copy(k, h).start()
+        for k, h in ((1, 0), (2, 1), (1, 1), (2, 0)):
+            back_copy(k, h).wait_recv()
+        finish(partners)
+        for h in range(2):
+            forward(h).wait_send()
+            across(h).wait_send()
+            for k in partners:
+                out_copy(k, h).wait_send()
+                back_copy(k, h).wait_send()
+        return
+
+    for k in partners:
+        for h in range(pieces):
+            out_copy(k, h).start()
     own.wait()
 
-    def step(k, carry):
+    def step(i, carry):
+        k = i // pieces
+        h = i % pieces
+
         @pl.when(k > 0)
         def _():
-            out_copy(k).wait_recv()
-
-        block_step(k, flip(mp, k, groups))
+            out_copy(k, h).wait_recv()
+
+        block_step(i, flip(mp, k, groups) * pieces + h)
 
         @pl.when(k > 0)
         def _():
-            back_copy(k).start()
+            back_copy(k, h).start()
 
         return carry
 
-    lax.fori_loop(0, groups, step, 0)
-    for k in range(1, groups):
-        back_copy(k).wait_recv()
-    finish()
-    for k in range(1, groups):
-        out_copy(k).wait_send()
-        back_copy(k).wait_send()
-
-
-def sum_parts(groups, parts, backs, rows):
-    total = parts[0, rows, :].astype(jnp.float32)
-    for k in range(1, groups):
-        total = total + backs[k, rows, :].astype(jnp.float32)
-    return total
+    lax.fori_loop(0, groups * pieces, step, 0)
+    for k in partners:
+        for h in range(pieces):
+            back_copy(k, h).wait_recv()
+    finish(partners)
+    for k in partners:
+        for h in range(pieces):
+            out_copy(k, h).wait_send()
+            back_copy(k, h).wait_send()
+
+
+def finish_rows(x_ref, parts, backs, partners, write):
+    pieces, row_count = x_ref.shape[:2]
+    rows_tile = tile_of(row_count, 32)
+    for h in range(pieces):
+
+        def some(i, carry, h=h):
+            rows = pl.ds(pl.multiple_of(i * rows_tile, rows_tile), rows_tile)
+            total = parts[h, rows, :].astype(jnp.float32)
+            for k in partners:
+                total = total + backs[k * pieces + h, rows, :].astype(jnp.float32)
+            write(h, rows, total)
+            return carry
+
+        lax.fori_loop(0, row_count // rows_tile, some, 0)
 
 
 def attention_kernel(
@@ -207,17 +331,18 @@
     blocks,
     parts,
     backs,
+    relay,
     attended_ref,
     *sems,
 ):
-    row_count, depth = x_ref.shape
+    row_count, depth = x_ref.shape[1:]
     width = w_ref.shape[2]
     heads = width // HEAD
     scale = 1.0 / math.sqrt(HEAD)
     tile = tile_of(depth, 256)
 
-    def block_step(k, source):
-        x = blocks[k]
+    def block_step(at_block, source):
+        x = blocks[at_block]
 
         def project(t):
             y = jnp.dot(x, w_ref[t], preferred_element_type=jnp.float32)
@@ -247,7 +372,7 @@
 
         def column(t, carry):
             at = pl.ds(pl.multiple_of(t * tile, tile), tile)
-            parts[k, :, at] = lax.dot_general(
+            parts[at_block, :, at] = lax.dot_general(
                 attended_ref[...],
                 w_ref[3, at, :],
                 (((1,), (1,)), ((), ())),
@@ -257,23 +382,15 @@
 
         lax.fori_loop(0, depth // tile, column, 0)
 
-    def finish():
-        rows_tile = tile_of(row_count, 32)
-
-        def some(i, carry):
-            rows = pl.ds(pl.multiple_of(i * rows_tile, rows_tile), rows_tile)
-            residual = (
-                stream_ref[rows, :].astype(jnp.float32)
-                + sum_parts(groups, parts, backs, rows)
-                + bias_ref[...]
-            )
-            residual_ref[rows, :] = residual
-            normed_ref[rows, :] = norm_rows(residual, gain_ref[...], shift_ref[...])
-            return carry
-
-        lax.fori_loop(0, row_count // rows_tile, some, 0)
-
-    exchange(groups, x_ref, blocks, parts, backs, sems, block_step, finish)
+    def finish(partners):
+        def write(h, rows, total):
+            residual = stream_ref[h, rows, :].astype(jnp.float32) + total + bias_ref[...]
+            residual_ref[h, rows, :] = residual
+            normed_ref[h, rows, :] = norm_rows(residual, gain_ref[...], shift_ref[...])
+
+        finish_rows(x_ref, parts, backs, partners, write)
+
+    exchange(groups, x_ref, blocks, parts, backs, relay, sems, block_step, finish)
 
 
 def mlp_kernel(
@@ -288,18 +405,19 @@
     blocks,
     parts,
     backs,
+    relay,
     hidden_ref,
     *sems,
 ):
-    row_count, depth = x_ref.shape
+    row_count, depth = x_ref.shape[1:]
     width = up_ref.shape[1]
     tile = tile_of(depth, 256)
     up_tile = tile_of(width, 256)
 
-    def block_step(k, source):
+    def block_step(at_block, source):
         def up(t, carry):
             at = pl.ds(pl.multiple_of(t * up_tile, up_tile), up_tile)
-            y = jnp.dot(blocks[k], up_ref[:, at], preferred_element_type=jnp.float32) + b_ref[:, at]
+            y = jnp.dot(blocks[at_block], up_ref[:, at], preferred_element_type=jnp.float32) + b_ref[:, at]
             y = 0.5 * y * (1.0 + lax.erf(y * math.sqrt(0.5)))
             hidden_ref[:, at] = y.astype(jnp.bfloat16)
             return carry
@@ -308,41 +426,42 @@
 
         def column(t, carry):
             at = pl.ds(pl.multiple_of(t * tile, tile), tile)
-            parts[k, :, at] = jnp.dot(
-                hidden_ref[...], down_ref[:, at], preferred_element_type=jnp.float32
+            parts[at_block, :, at] = lax.dot_general(
+                hidden_ref[...],
+                down_ref[at, :],
+                (((1,), (1,)), ((), ())),
+                preferred_element_type=jnp.float32,
             ).astype(jnp.bfloat16)
             return carry
 
         lax.fori_loop(0, depth // tile, column, 0)
 
-    def finish():
-        rows_tile = tile_of(row_count, 32)
-
-        def some(i, carry):
-            rows = pl.ds(pl.multiple_of(i * rows_tile, rows_tile), rows_tile)
-            out_ref[rows, :] = (
-                residual_ref[rows, :] + sum_parts(groups, parts, backs, rows) + bias_ref[...]
-            ).astype(jnp.bfloat16)
-            return carry
-
-        lax.fori_loop(0, row_count // rows_tile, some, 0)
-
-    exchange(groups, x_ref, blocks, parts, backs, sems, block_step, finish)
+    def finish(partners):
+        def write(h, rows, total):
+            out_ref[h, rows, :] = (residual_ref[h, rows, :] + total + bias_ref[...]).astype(
+                jnp.bfloat16
+            )
+
+        finish_rows(x_ref, parts, backs, partners, write)
+
+    exchange(groups, x_ref, blocks, parts, backs, relay, sems, block_step, finish)
 
 
 def exchange_call(kernel, groups, args, outs, width, collective_id, name):
-    row_count, depth = args[0].shape
+    pieces, row_count, depth = args[0].shape
     vmem = pl.BlockSpec(memory_space=pltpu.VMEM)
-    many = pltpu.SemaphoreType.DMA((groups,))
+    many = pltpu.SemaphoreType.DMA((groups * pieces,))
+    buffer = pltpu.VMEM((groups * pieces, row_count, depth), jnp.bfloat16)
     return pl.pallas_call(
         functools.partial(kernel, groups),
         out_shape=outs,
         in_specs=[vmem] * len(args),
         out_specs=jax.tree.map(lambda _: vmem, outs),
         scratch_shapes=[
-            pltpu.VMEM((groups, row_count, depth), jnp.bfloat16),
-            pltpu.VMEM((groups, row_count, depth), jnp.bfloat16),
-            pltpu.VMEM((groups, row_count, depth), jnp.bfloat16),
+            buffer,
+            buffer,
+            buffer,
+            pltpu.VMEM((pieces, row_count, depth), jnp.bfloat16),
             pltpu.VMEM((row_count, width), jnp.bfloat16),
             pltpu.SemaphoreType.DMA,
             many,
@@ -390,14 +509,14 @@
 
     attention_shard = jnp.concatenate([w_qkv[0], w_o[0].T[None]], axis=0)
     w_attention = lax.all_gather(attention_shard, "dp", axis=1, tiled=True)
-    w_up_full = lax.all_gather(w_up[0], "dp", axis=0, tiled=True)
-    w_down_full = lax.all_gather(w_down[0], "dp", axis=1, tiled=True)
 
     chosen = (keep[:, :, None] == jnp.arange(patch_count, dtype=jnp.int32)).astype(jnp.bfloat16)
     tokens = (
         jnp.einsum("ijp,ipd->ijd", chosen, patches, preferred_element_type=f32)
         + jnp.einsum("ijp,pd->ijd", chosen, position, preferred_element_type=f32)
     ).astype(jnp.bfloat16)
+    tokens, w_up_shard = lax.optimization_barrier((tokens, w_up[0]))
+    w_up_full = lax.all_gather(w_up_shard, "dp", axis=0, tiled=True)
 
     first_image = dp_index * images_here
     group_counts = lax.dynamic_slice_in_dim(counts, first_image, images_here)
@@ -419,22 +538,22 @@
     featured = lax.all_to_all(
         tokens.reshape(-1, column_count), "mp", split_axis=1, concat_axis=0, tiled=True
     )
+    featured, w_down_shard = lax.optimization_barrier((featured, w_down[0]))
+    w_down_rows = lax.all_gather(w_down_shard, "dp", axis=1, tiled=True).T
     feature_count = featured.shape[1]
     placing = (jnp.arange(pack_rows, dtype=jnp.int32)[:, None] == target[None, :]).astype(
         jnp.bfloat16
     )
     packed = jnp.dot(placing, featured, preferred_element_type=f32).astype(jnp.bfloat16)
-    arrived = route(
-        packed.reshape(shard_count, slot_rows, feature_count), shard_count, group_size
-    )
-    per = shard_count // group_size
-    stream = (
-        arrived.reshape(per, group_size, slot_rows, feature_count)
-        .transpose(0, 2, 1, 3)
-        .reshape(local_rows, column_count)
-    )
-    normed = norm_rows(stream.astype(f32), ln_gain[0, 0], ln_bias[0, 0])
-    by_group = labels.reshape(group_size, local_rows)
+    stream, normed = route(
+        packed.reshape(shard_count, slot_rows, feature_count),
+        ln_gain[:, 0],
+        ln_bias[:, 0],
+        shard_count,
+        group_size,
+    )
+    pieces = stream.shape[0]
+    by_piece = labels.reshape(group_size * pieces, local_rows // pieces)
     residual, normed_mlp = exchange_call(
         attention_kernel,
         group_size,
@@ -443,15 +562,15 @@
             stream,
             w_attention,
             b_qkv[0][:, None, :],
-            by_group[:, :, None],
-            by_group[:, None, :],
+            by_piece[:, :, None],
+            by_piece[:, None, :],
             b_o,
             ln_gain[:, 1],
             ln_bias[:, 1],
         ),
         (
-            jax.ShapeDtypeStruct((local_rows, column_count), f32),
-            jax.ShapeDtypeStruct((local_rows, column_count), jnp.bfloat16),
+            jax.ShapeDtypeStruct(stream.shape, f32),
+            jax.ShapeDtypeStruct(stream.shape, jnp.bfloat16),
         ),
         w_attention.shape[2],
         1,
@@ -460,12 +579,12 @@
     stream = exchange_call(
         mlp_kernel,
         group_size,
-        (normed_mlp, residual, w_up_full, b_up, w_down_full, b_down),
-        jax.ShapeDtypeStruct((local_rows, column_count), jnp.bfloat16),
+        (normed_mlp, residual, w_up_full, b_up, w_down_rows, b_down),
+        jax.ShapeDtypeStruct(stream.shape, jnp.bfloat16),
         w_up_full.shape[1],
         2,
         "mlp",
-    )
+    ).reshape(local_rows, column_count)
     own_labels = lax.dynamic_slice_in_dim(labels, mp_index * local_rows, local_rows)
     return jnp.where(own_labels[:, None] >= 0, stream, jnp.zeros_like(stream))
 

time: 275 us -> 219 us (0.80)
  Pallas kernels: 182 us -> 159 us
  waiting for transfers between devices: 36.9 us -> 17.4 us
  local copies, waits for them, and re-layouts: 20.5 us -> 12.5 us
  other arithmetic: 10.2 us -> 3.75 us
    pallas_call x2, Pallas kernels: 157 us -> 132 us  [exchange_call(): pl.pallas_call(functools.partial(kernel, groups), out_shape=outs, in_spec...]
    all_gather x1, waiting for transfers between devices: 21.2 us -> 0.02 us  [per_device(): w_attention = lax.all_gather(attention_shard, 'dp', axis=1, tiled=True)]
    reduce_sum x2 -> x0, other arithmetic: 6.11 us -> none  [the longest x1 3.67 us: norm_rows(): spread = jnp.mean(centred * centred, axis=-1, keepdims=True)]
    all_gather x1 -> x0, local copies, waits for them, and re-layouts: 5.68 us -> none  [per_device(): w_down_full = lax.all_gather(w_down[0], 'dp', axis=1, tiled=True)]
    reshape x2 -> x0, local copies, waits for them, and re-layouts: 3.51 us -> none  [the longest x1 2.05 us: per_device(): stream = arrived.reshape(per, group_size, slot_rows, feature_count).trans...]
    all_gather x2, waiting for transfers between devices: 0.02 us -> 2.96 us  [the longest x1 2.96 us: per_device(): w_down_rows = lax.all_gather(w_down_shard, 'dp', axis=1, tiled=True).T]
  transfers between devices with their start and end apart: 4 -> 4, of which waited for: 2 -> 2; matrix products, arithmetic and copies ran while one was open for 11% -> 7% of each run, Pallas kernels for 38% -> 45%
where the time goes in v2:
time: 219 us
  Pallas kernels  159 us (73%)
  waiting for transfers between devices  17.4 us (8%)
  between operations  13.3 us (6%)
  local copies, waits for them, and re-layouts  12.5 us (6%)
  matrix products  7.64 us (3%)
  starting transfers between devices  5.38 us (2%)
  other arithmetic  3.75 us (2%)
    pallas_call x2, Pallas kernels, exchange_call(): pl.pallas_call(functools.partial(kernel, groups), out_shape=outs, in_spec...  132 us
    pallas_call x1, Pallas kernels, route(): pl.pallas_call(functools.partial(route_kernel, shards, groups), out_shape...  26.8 us
    all_to_all x1, waiting for transfers between devices, per_device(): lax.all_to_all(tokens.reshape(-1, column_count), 'mp', split_axis=1, conc...  14.4 us
    all_to_all x3, local copies, waits for them, and re-layouts, per_device(): lax.all_to_all(tokens.reshape(-1, column_count), 'mp', split_axis=1, conc...  5.57 us
    all_to_all x1, starting transfers between devices, per_device(): lax.all_to_all(tokens.reshape(-1, column_count), 'mp', split_axis=1, conc...  5.33 us
  transfers between devices with their start and end apart: 4, of which 2 were waited for; matrix products, arithmetic and copies ran while one was open for 7% of the time, Pallas kernels for 45%

profile of v2, /device:TPU:0, one launch (start us, length us, event | category | flops | bytes accessed | tf_op | source)
XLA Modules:
  0.0 218.6 jit_solution(1761831950543724130)
XLA Ops:
  6.5 2.0 pad_maximum_fusion
  8.5 0.0 all-gather.4.cloned.1.call-update
  8.6 0.0 all-gather.6.cloned.1.call-start
  8.6 3.6 %fusion.5 = f32[8,64,1280]{2,1,0:T(8,128)S(1)} fusion(bf16[8,256,1280]{2,1,0:T(8,128)(2,1)} %param.15, s32[8,64]{1,0:T(8,128)} %param.17), kind=kOutput, calls=%fused_computation.10 | convolution fusion | flops 335675392 | bytes 7866368 | tf_op jit(solution)/shard_map/ijp,ipd->ijd/dot_general | solution.py:515
  12.2 0.6 fusion.2
  12.8 0.0 all-gather.6.cloned.1.call-update
  12.8 1.8 all_to_all.14
  14.6 2.5 %copy.24 = bf16[512,4,320]{0,2,1:T(8,128)(2,1)} copy(bf16[512,4,320]{2,1,0:T(4,128)(2,1)S(1)} %all_to_all.14) | data formatting | bytes 2621440 | tf_op jit(solution)/shard_map/all_to_all | solution.py:538
  17.0 5.3 %all-to-all-start = ((bf16[512,4,320]{0,2,1:T(8,128)(2,1)}), bf16[512,4,320]{0,2,1:T(8,128)(2,1)S(1)}, u32[]{:S(2)}, u32[]{:S(2)}) async-start(bf16[512,4,320]{0,2,1:T(8,128)(2,1)} %copy.24), calls=%async_computation | async-start | bytes 2621440 | tf_op jit(solution)/shard_map/all_to_all | solution.py:538
  22.4 0.5 select_reduce_fusion
  22.9 0.5 sub.30.label_col_ref
  23.4 0.1 sub.29.label_row_ref
  23.5 0.1 dynamic_slice.10
  23.5 0.1 subtract_subtract_fusion
  23.6 0.1 add_select_fusion
  23.7 0.1 select_n.36
  23.8 0.1 dynamic-slice_compare_fusion
  23.9 0.6 slice_bitcast_fusion
  24.5 14.4 %all-to-all-done = bf16[512,4,320]{0,2,1:T(8,128)(2,1)S(1)} async-done(((bf16[512,4,320]{0,2,1:T(8,128)(2,1)}), bf16[512,4,320]{0,2,1:T(8,128)(2,1)S(1)}, u32[]{:S(2)}, u32[]{:S(2)}) %all-to-all-start) | async-done | bytes 1310752 | tf_op jit(solution)/shard_map/all_to_all | solution.py:538
  38.8 1.3 copy.28
  40.2 3.5 %fusion.3 = bf16[1280,320]{0,1:T(8,128)(2,1)S(1)} fusion(bf16[2048,320]{0,1:T(8,128)(2,1)} %bitcast.31, s32[2048]{0:T(1024)S(1)} %select_n.36), kind=kOutput, calls=%fused_computation.5 | convolution fusion | flops 1680752640 | bytes 2138112 | tf_op jit(solution)/shard_map/dot_general | solution.py:547
  43.7 1.3 copy.26
  45.0 26.8 %route.1 = (bf16[2,160,1280]{2,1,0:T(8,128)(2,1)}, bf16[2,160,1280]{2,1,0:T(8,128)(2,1)}) custom-call(bf16[8,160,320]{2,1,0:T(8,128)(2,1)} %bitcast.32, f32[1,1280]{1,0:T(1,128)} %get-tuple-element.25.gain_ref, f32[1,1280]{1,0:T(1,128)} %get-tuple-element.22.shift_ref), custom_call_target="tpu_custom_call" | custom-call | flops 15000000512 | tf_op jit(solution)/shard_map/route/pallas_call | solution.py:141
  71.9 0.0 all-gather.4.cloned.1.call-done.w_ref
  71.9 1.1 copy-done.5
  73.1 1.1 copy-done.6
  74.2 70.5 %attention.1 = (f32[2,160,1280]{2,1,0:T(8,128)S(1)}, bf16[2,160,1280]{2,1,0:T(8,128)(2,1)S(1)}) custom-call(bf16[2,160,1280]{2,1,0:T(8,128)(2,1)S(1)} %copy-done.6, bf16[2,160,1280]{2,1,0:T(8,128)(2,1)S(1)} %copy-done.5, bf16[4,1280,320]{2,1,0:T(8,128)(2,1)} %all-gather.4.cloned.1.call-done.w_ref, f32[3,1,320]{2,1,0:T(1,128)S(1)} %bitcast.29, ...), custom_call_target="tpu_custom_call" | custom-call | flops 49999998976 | tf_op jit(solution)/shard_map/attention/pallas_call | solution.py:455
  144.8 0.9 copy-done.7
  145.6 3.0 %all-gather.8.cloned.1.call-done = bf16[1280,1280]{0,1:T(8,128)(2,1)} async-done(((bf16[1280,160]{0,1:T(8,128)(2,1)}), bf16[1280,1280]{0,1:T(8,128)(2,1)}) %all-gather.8.cloned.1.call-update) | async-done | bytes 3276816 | tf_op jit(solution)/shard_map/all_gather | solution.py:542
  148.6 1.1 copy-done.8
  149.7 61.2 %mlp.1 = bf16[2,160,1280]{2,1,0:T(8,128)(2,1)S(1)} custom-call(bf16[2,160,1280]{2,1,0:T(8,128)(2,1)S(1)} %copy-done.8, f32[2,160,1280]{2,1,0:T(8,128)S(1)} %get-tuple-element.18.residual_ref, bf16[1280,1280]{1,0:T(8,128)(2,1)} %all-gather.6.cloned.1.call-done.up_ref, f32[1,1280]{1,0:T(1,128)S(1)} %copy-done.2, bf16[1280,1280]{1,0:T(8,128)(2,1)} %bitcast.37, ...), custom_call_target="tpu_custom_call" | custom-call | flops 49999998976 | tf_op jit(solution)/shard_map/mlp/pallas_call | solution.py:455
  211.0 1.1 bitcast_select_fusion
  (32 shorter events, 0.1 us)
Async XLA Ops:
  6.5 5.6 %copy-start = (bf16[256,1280]{1,0:T(8,128)(2,1)S(1)}, bf16[256,1280]{1,0:T(8,128)(2,1)}, u32[]{:S(2)}) copy-start(bf16[256,1280]{1,0:T(8,128)(2,1)} %param.16) | copy-start | bytes 1966084
  6.5 65.3 %all-gather.4.cloned.1.call-start = ((), (), s32[]{:S(2)}) async-start(), calls=%async_computation.1 | async-start | bytes 4423680 | tf_op jit(solution)/shard_map/all_gather | solution.py:511
  8.5 3.7 %copy-start.9 = (s32[8,64]{1,0:T(8,128)S(1)}, s32[8,64]{1,0:T(8,128)}, u32[]{:S(2)}) copy-start(s32[8,64]{1,0:T(8,128)} %param.17) | copy-start | bytes 6148
  8.6 137.1 %all-gather.6.cloned.1.call-start = ((), (), s32[]{:S(2)}) async-start(), calls=%async_computation.2 | async-start | bytes 3686400 | tf_op jit(solution)/shard_map/all_gather | solution.py:519
  17.0 5.3 %copy-start.12 = (s32[256]{0:T(256)S(1)}, s32[256]{0:T(256)}, u32[]{:S(2)}) copy-start(s32[256]{0:T(256)} %param.19) | copy-start | bytes 3076
  17.0 5.3 %copy-start.13 = (s32[256]{0:T(256)S(1)}, s32[256]{0:T(256)}, u32[]{:S(2)}) copy-start(s32[256]{0:T(256)} %param.18) | copy-start | bytes 3076
  17.0 6.8 %copy-start.10 = (f32[1,2,1280]{2,1,0:T(2,128)S(1)}, f32[1,2,1280]{2,1,0:T(2,128)}, u32[]{:S(2)}) copy-start(f32[1,2,1280]{2,1,0:T(2,128)} %param.21) | copy-start | bytes 30724
  17.0 6.8 %copy-start.11 = (f32[1,2,1280]{2,1,0:T(2,128)S(1)}, f32[1,2,1280]{2,1,0:T(2,128)}, u32[]{:S(2)}) copy-start(f32[1,2,1280]{2,1,0:T(2,128)} %param.20) | copy-start | bytes 30724
  17.0 21.8 %all-to-all-start = ((bf16[512,4,320]{0,2,1:T(8,128)(2,1)}), bf16[512,4,320]{0,2,1:T(8,128)(2,1)S(1)}, u32[]{:S(2)}, u32[]{:S(2)}) async-start(bf16[512,4,320]{0,2,1:T(8,128)(2,1)} %copy.24), calls=%async_computation | async-start | bytes 2621440 | tf_op jit(solution)/shard_map/all_to_all | solution.py:538
  22.4 126.2 %all-gather.8.cloned.1.call-start = ((), (), s32[]{:S(2)}) async-start(), calls=%async_computation.3 | async-start | bytes 3686400 | tf_op jit(solution)/shard_map/all_gather | solution.py:542
  45.0 26.9 %copy-start.1 = (f32[1,1280]{1,0:T(1,128)S(1)}, f32[1,1280]{1,0:T(1,128)}, u32[]{:S(2)}) copy-start(f32[1,1280]{1,0:T(1,128)} %bias_ref.2) | copy-start | bytes 15364
  45.0 26.9 %copy-start.4 = (f32[1,3,320]{2,0,1:T(1,128)S(1)}, f32[1,3,320]{2,0,1:T(1,128)}, u32[]{:S(2)}) copy-start(f32[1,3,320]{2,0,1:T(1,128)} %param.23) | copy-start | bytes 11524
  71.9 1.1 copy-start.5
  73.1 1.1 copy-start.6
  74.2 74.4 %copy-start.2 = (f32[1,1280]{1,0:T(1,128)S(1)}, f32[1,1280]{1,0:T(1,128)}, u32[]{:S(2)}) copy-start(f32[1,1280]{1,0:T(1,128)} %b_ref.1) | copy-start | bytes 15364
  74.2 74.4 %copy-start.3 = (f32[1,1280]{1,0:T(1,128)S(1)}, f32[1,1280]{1,0:T(1,128)}, u32[]{:S(2)}) copy-start(f32[1,1280]{1,0:T(1,128)} %bias_ref.3) | copy-start | bytes 15364
  144.7 0.9 copy-start.7
  148.6 1.1 copy-start.8
Sparse Core Ops, SparseCore 0:
  8.9 56.6 all-gather.3
  67.3 40.7 all-gather.5
  109.8 38.7 all-gather.7
